TPU v7x, 256 devices: a whole 4x4x8 slice. The times are simulated.
256 devices in a mesh: dp: 32 (over x, z_lo, core), head: 8 (over y, z_hi).
Axes of the slice: x: 4, y: 4, z: 8 (z_hi: 2, z_lo: 4; z = z_hi * 4 + z_lo), core: 2. Of those that a mesh axis runs over, the one named last changes fastest.
Arguments:
- frames_in: bfloat16 [32, 8, 320, 640], P('dp', 'head'), may hold values from -6 to 6
- ln1_gain: float32 [1280], replicated, may hold values from 0.25 to 1.75
- ln1_bias: float32 [1280], replicated, may hold values from -3 to 3
- qkv_weight: bfloat16 [1280, 3, 1024], P('dp', None, 'head'), may hold values from -0.1875 to 0.1875
- qv_bias: float32 [2, 1024], P(None, 'head'), may hold values from -3 to 3
- out_weight: bfloat16 [1024, 1280], P(('head', 'dp')), may hold values from -0.1875 to 0.1875
- out_bias: float32 [1280], P('head'), may hold values from -3 to 3
- ln2_gain: float32 [1280], replicated, may hold values from 0.25 to 1.75
- ln2_bias: float32 [1280], replicated, may hold values from -3 to 3
- fc1_weight: bfloat16 [1280, 5120], P('dp', 'head'), may hold values from -0.15625 to 0.15625
- fc1_bias: float32 [5120], P('head'), may hold values from -3 to 3
- fc2_weight: bfloat16 [5120, 1280], P(('head', 'dp')), may hold values from -0.078125 to 0.078125
- fc2_bias: float32 [1280], P('head'), may hold values from -3 to 3
- server_of_clip: int32 [32], replicated, may hold values from 0 to 7
Outputs:
- encoded: bfloat16 [32, 8, 320, 640], P('dp', 'head')
All inputs are finite; a program needn't handle non-finite values.
Results may differ from a plain program's by a relative error of at most 0.014.
Values may be sent and summed in bfloat16 or wider, within the bound.
No kernel may reach another device: no remote copies, remote signals or barrier semaphores. Data moves between devices by JAX's collectives and lax.ppermute only.
A program may use at most 64 MiB of HBM per device.

v0:
```python
import jax
import jax.numpy as jnp
from jax import lax
from jax.sharding import Mesh
from jax.sharding import PartitionSpec as P

HDIM = 64
HEAD = ("head_0", "head_1")
HEAD_DP = ("head_0", "head_1", "dp")
epsilon = 1e-05


def laid_out(blocks, dim):
    dims = list(blocks.shape[1:])
    dims[dim] *= blocks.shape[0]
    return jnp.moveaxis(blocks, 0, dim).reshape(dims)


def sent_to_all(value, axis):
    copies = jnp.broadcast_to(value, (lax.axis_size(axis), *value.shape))
    return lax.all_to_all(copies, axis, split_axis=0, concat_axis=0, tiled=True)


def gather_directly(value, axis, dim):
    return laid_out(sent_to_all(value, axis), dim)


def own_rows(terms, axes):
    total = terms.astype(jnp.bfloat16)
    for axis in axes:
        total = lax.psum_scatter(total, axis, scatter_dimension=0, tiled=True)
    return total.astype(jnp.float32)


def layer_norm(matrix, gain_row, shift_row):
    floats = matrix.astype(jnp.float32)
    center = jnp.mean(floats, axis=-1, keepdims=True)
    spread = jnp.mean(jnp.square(floats - center), axis=-1, keepdims=True)
    return ((floats - center) * lax.rsqrt(spread + epsilon) * gain_row + shift_row).astype(
        jnp.bfloat16
    )


def normalize(residual_in, gain_row, shift_row):
    whole_rows = lax.all_gather(residual_in, HEAD, axis=1, tiled=True)
    return layer_norm(whole_rows, gain_row, shift_row)


def attend(queries, key_rows, value_rows):

    def single(triple):
        query_head, key_head, value_head = triple
        scores = jnp.dot(query_head, key_head.T, preferred_element_type=jnp.float32)
        maxima = jnp.max(scores, axis=-1, keepdims=True)
        weights = jnp.exp(scores - maxima)
        probability = (weights / jnp.sum(weights, axis=-1, keepdims=True)).astype(jnp.bfloat16)
        return jnp.dot(probability, value_head, preferred_element_type=jnp.float32).astype(
            jnp.bfloat16
        )

    per_head = lax.map(
        single,
        (jnp.swapaxes(queries, 0, 1), jnp.swapaxes(key_rows, 0, 1), jnp.swapaxes(value_rows, 0, 1)),
    )
    return jnp.swapaxes(per_head, 0, 1).reshape(queries.shape[0], -1)


def slot_order(server_list):
    clip_count = server_list.shape[0]
    indices = jnp.arange(clip_count, dtype=jnp.int32)
    earlier = (server_list[None, :] < server_list[:, None]) | (
        server_list[None, :] == server_list[:, None]
    ) & (indices[None, :] < indices[:, None])
    slot_of = jnp.sum(earlier.astype(jnp.int32), axis=1)
    return jnp.sum(jnp.where(slot_of[None, :] == indices[:, None], indices[None, :], 0), axis=1)


def regroup(block_rows, clip_order):
    group_size = lax.axis_size("dp")
    piece_rows = block_rows.reshape(group_size, -1)
    shuffled = lax.all_to_all(piece_rows, "dp", split_axis=0, concat_axis=0, tiled=True)
    picked = jnp.take(shuffled, clip_order, axis=0)
    returned = lax.all_to_all(picked, "dp", split_axis=0, concat_axis=0, tiled=True)
    return returned.reshape(block_rows.shape)


def block_term(operand, weight_rows, row_count, frame_count, local_width):
    blocks = row_count // frame_count
    product = jnp.dot(operand, weight_rows, preferred_element_type=jnp.float32)
    return (
        product.reshape(frame_count, blocks, local_width)
        .transpose(1, 0, 2)
        .reshape(blocks * frame_count, local_width)
    )


def on_device(
    frames_in,
    ln1_gain,
    ln1_bias,
    qkv_weight,
    qv_bias,
    out_weight,
    out_bias,
    ln2_gain,
    ln2_bias,
    fc1_weight,
    fc1_bias,
    fc2_weight,
    fc2_bias,
    server_of_clip,
):
    clip_order = slot_order(server_of_clip)
    group_rows = frames_in.shape[2]
    local_width = frames_in.shape[3] // 4
    frame_count = group_rows * 4
    residual_in = frames_in[0, 0].reshape(frame_count, local_width)
    residual_in = regroup(residual_in, clip_order)
    head_count = lax.axis_size(HEAD)
    normed_one = normalize(residual_in, ln1_gain, ln1_bias)
    column_count = qkv_weight.shape[2]
    weight_piece = lax.all_gather(qkv_weight, "dp", axis=0, tiled=True)
    operand = normed_one
    projected = jnp.dot(
        operand, weight_piece.reshape(weight_piece.shape[0], -1), preferred_element_type=jnp.float32
    ).reshape(frame_count, 3, column_count)
    queries = (
        ((projected[:, 0] + qv_bias[0]) * HDIM ** (-0.5))
        .astype(jnp.bfloat16)
        .reshape(frame_count, -1, HDIM)
    )
    key_rows = projected[:, 1].astype(jnp.bfloat16).reshape(frame_count, -1, HDIM)
    value_rows = (projected[:, 2] + qv_bias[1]).astype(jnp.bfloat16).reshape(frame_count, -1, HDIM)
    context = attend(queries, key_rows, value_rows)
    output_rows = lax.all_gather(out_weight, "dp", axis=0, tiled=True)
    carried = residual_in.astype(jnp.float32) + out_bias
    whole_context = gather_directly(context, HEAD, 1)
    split_rows = output_rows.reshape(output_rows.shape[0], head_count, local_width)
    feature_columns = lax.all_to_all(
        split_rows, HEAD, split_axis=1, concat_axis=0, tiled=True
    ).reshape(-1, local_width)
    attended = (
        carried + jnp.dot(whole_context, feature_columns, preferred_element_type=jnp.float32)
    ).astype(jnp.bfloat16)
    normed_two = normalize(attended, ln2_gain, ln2_bias)
    operand = normed_two
    hidden_sums = jnp.dot(
        operand, gather_directly(fc1_weight, "dp", 0), preferred_element_type=jnp.float32
    )
    hidden = jax.nn.gelu(hidden_sums + fc1_bias, approximate=False).astype(jnp.bfloat16)
    down_rows = lax.all_gather(fc2_weight, "dp", axis=0, tiled=True)
    kept = attended.astype(jnp.float32) + fc2_bias
    layer_out = (
        kept
        + own_rows(
            block_term(
                hidden, down_rows, frame_count * lax.axis_size(HEAD), frame_count, local_width
            ),
            HEAD,
        )
    ).astype(jnp.bfloat16)
    return layer_out.reshape(1, 1, group_rows, 4 * local_width)


def solution(mesh):
    torus = Mesh(mesh.devices.reshape(mesh.shape["dp"], 4, 2), ("dp", "head_0", "head_1"))
    return jax.shard_map(
        on_device,
        mesh=torus,
        in_specs=(
            P("dp", HEAD, None, None),
            P(),
            P(),
            P("dp", None, HEAD),
            P(None, HEAD),
            P(HEAD_DP, None),
            P(HEAD),
            P(),
            P(),
            P("dp", HEAD),
            P(HEAD),
            P(HEAD_DP, None),
            P(HEAD),
            P(),
        ),
        out_specs=P("dp", HEAD, None, None),
        check_vma=False,
    )
```

profile of v0, /device:TPU:2, one launch (start us, length us, event | category | flops | bytes accessed | tf_op | source)
XLA Modules:
  0.0 519.4 jit_solution(1292017763583869009)
XLA Ops:
  7.4 2.4 all_to_all.38
  10.3 3.1 reduce.9
  14.3 9.1 %all-to-all-start = ((bf16[32,2,3200]{2,1,0:T(2,128)(2,1)}), bf16[32,2,3200]{2,1,0:T(2,128)(2,1)S(1)}, u32[]{:S(2)}, u32[]{:S(2)}) async-start(bf16[32,2,3200]{2,1,0:T(2,128)(2,1)} %reshape.166), calls=%async_computation | async-start | bytes 819200 | tf_op jit(solution)/shard_map/all_to_all | solution.py:81
  23.7 11.2 %all-to-all-done = bf16[32,2,3200]{2,1,0:T(2,128)(2,1)S(1)} async-done(((bf16[32,2,3200]{2,1,0:T(2,128)(2,1)}), bf16[32,2,3200]{2,1,0:T(2,128)(2,1)S(1)}, u32[]{:S(2)}, u32[]{:S(2)}) %all-to-all-start) | async-done | bytes 409632 | tf_op jit(solution)/shard_map/all_to_all | solution.py:81
  37.2 17.8 %all_to_all.44 = bf16[32,2,3200]{2,1,0:T(2,128)(2,1)S(1)} all-to-all(bf16[32,2,3200]{2,1,0:T(2,128)(2,1)S(1)} %reshape.168), channel_id=1, replica_groups=mesh['dp'=32,'head_0'=4,'head_1'=2] {'dp'}, dimensions={0} | all-to-all | bytes 819200 | tf_op jit(solution)/shard_map/all_to_all | solution.py:83
  55.4 2.4 reduce
  59.7 38.8 %all-gather = bf16[32,4,1280]{2,1,0:T(4,128)(2,1)S(1)} all-gather(bf16[1,4,1280]{2,1,0:T(4,128)(2,1)S(1)} %bitcast.96), channel_id=1, replica_groups=mesh['dp'=32,'head_0'=4,'head_1'=2] {'dp'}, dimensions={0}, use_global_device_ids=true | all-gather | bytes 337920 | tf_op jit(solution)/shard_map/all_gather | solution.py:135
  100.3 7.2 %all-to-all-start.3 = ((bf16[128,8,160]{0,2,1:T(8,128)(2,1)}), bf16[128,8,160]{0,2,1:T(8,128)(2,1)S(1)}, u32[]{:S(2)}, u32[]{:S(2)}) async-start(bf16[128,8,160]{0,2,1:T(8,128)(2,1)} %copy.63), calls=%async_computation.3 | async-start | bytes 655360 | tf_op jit(solution)/shard_map/all_to_all | solution.py:139
  107.5 64.6 %all_gather.16 = bf16[1280,3,128]{2,0,1:T(8,128)(2,1)S(1)} all-gather(bf16[40,3,128]{2,0,1:T(8,128)(2,1)S(1)} %copy-done.8), channel_id=1, replica_groups=mesh['dp'=32,'head_0'=4,'head_1'=2] {'dp'}, dimensions={0}, use_global_device_ids=true | all-gather | bytes 1013760 | tf_op jit(solution)/shard_map/all_gather | solution.py:122
  172.9 2.6 convert_reduce_fusion.1
  176.7 1.8 fusion.41
  179.1 1.5 copy.62
  180.9 2.4 fusion.50
  183.4 8.4 %while.10 = (s32[]{:T(128)}, bf16[2,1280,64]{1,2,0:T(8,128)(2,1)}, bf16[2,1280,64]{2,1,0:T(8,128)(2,1)S(1)}, bf16[2,1280,64]{2,1,0:T(8,128)(2,1)S(1)}, bf16[2,1280,64]{2,1,0:T(8,128)(2,1)}, /*index=5*/s32[]{:T(128)}) while((s32[]{:T(128)}, bf16[2,1280,64]{1,2,0:T(8,128)(2,1)}, bf16[2,1280,64]{2,1,0:T(8,128)(2,1)S(1)}, ...), condition=%wide.region_7.8_spmd, body=%wide.region_4.7_spmd.sunk | while | flops 429340160 | bytes 24773784 | solution.py:61
  185.6 1.3 fusion.99
  189.8 1.3 fusion.99
  191.8 2.6 broadcast_in_dim.36
  194.4 8.3 %all-to-all-start.2 = ((bf16[8,1280,128]{1,2,0:T(8,128)(2,1)}), bf16[8,1280,128]{1,2,0:T(8,128)(2,1)S(1)}, u32[]{:S(2)}, u32[]{:S(2)}) async-start(bf16[8,1280,128]{1,2,0:T(8,128)(2,1)} %broadcast_in_dim.36), calls=%async_computation.2 | async-start | bytes 5242880 | tf_op jit(solution)/shard_map/all_to_all | solution.py:21
  204.2 61.5 %all-to-all-done.2 = bf16[8,1280,128]{1,2,0:T(8,128)(2,1)S(1)} async-done(((bf16[8,1280,128]{1,2,0:T(8,128)(2,1)}), bf16[8,1280,128]{1,2,0:T(8,128)(2,1)S(1)}, u32[]{:S(2)}, u32[]{:S(2)}) %all-to-all-start.2) | async-done | bytes 2621472 | tf_op jit(solution)/shard_map/all_to_all | solution.py:21
  265.7 2.3 fusion.46
  268.0 1.4 broadcast_in_dim.37
  269.4 12.6 %all-to-all-start.4 = ((bf16[32,40,640]{2,1,0:T(8,128)(2,1)}), bf16[32,40,640]{2,1,0:T(8,128)(2,1)}, u32[]{:S(2)}, u32[]{:S(2)}) async-start(bf16[32,40,640]{2,1,0:T(8,128)(2,1)} %broadcast_in_dim.37), calls=%async_computation.4 | async-start | bytes 3276800 | tf_op jit(solution)/shard_map/all_to_all | solution.py:21
  282.1 31.7 %all-gather.10.cloned.1.call-done = bf16[32,20,1280]{2,1,0:T(8,128)(2,1)} async-done(((bf16[1,20,1280]{2,1,0:T(8,128)(2,1)}), bf16[32,20,1280]{2,1,0:T(8,128)(2,1)}) %all-gather.10.cloned.1.call-update) | async-done | bytes 1638416 | tf_op jit(solution)/shard_map/all_gather | solution.py:151
  313.8 4.1 reshape.150
  317.9 93.8 %all-gather.8.cloned.1.call-done = bf16[1280,1280]{0,1:T(8,128)(2,1)} async-done(((bf16[1280,160]{0,1:T(8,128)(2,1)}), bf16[1280,1280]{0,1:T(8,128)(2,1)}) %all-gather.8.cloned.1.call-update) | async-done | bytes 3276816 | tf_op jit(solution)/shard_map/all_gather | solution.py:45
  411.8 2.6 convert_reduce_fusion
  415.6 15.6 %convolution_convert_fusion = bf16[1280,1280]{0,1:T(8,128)(2,1)} fusion(bf16[640,1280]{1,0:T(8,128)(2,1)} %reshape.150, bf16[1280,640]{1,0:T(8,128)(2,1)} %bitcast.24, bf16[1280,1280]{0,1:T(8,128)(2,1)S(1)} %copy-done.1, f32[1280]{0:T(1024)S(1)} %copy-done.15, f32[1280]{0:T(1024)S(1)} %copy-done.16, f32[1280]{0:T(1024)S(1)} %add_rsqrt_fusion, ...), kind=kOutput, calls=%fused_computation.25 | convolution fusion | flops 4259840000 | bytes 9853440 | tf_op jit(solution)/shard_map/dot_general | solution.py:89
  431.2 4.0 copy.71
  435.3 37.3 %reduce-scatter.3.cloned.1.call-done = bf16[2560,160]{0,1:T(8,128)(2,1)} async-done(((bf16[10240,160]{0,1:T(8,128)(2,1)}), bf16[2560,160]{0,1:T(8,128)(2,1)}) %reduce-scatter.3.cloned.1.call-update) | async-done | bytes 819216 | tf_op jit(solution)/shard_map/reduce_scatter | solution.py:31
  472.7 35.9 %reduce-scatter.5.cloned.1.call-done = bf16[1280,160]{0,1:T(8,128)(2,1)} async-done(((bf16[2560,160]{0,1:T(8,128)(2,1)}), bf16[1280,160]{0,1:T(8,128)(2,1)}) %reduce-scatter.5.cloned.1.call-update) | async-done | bytes 409616 | tf_op jit(solution)/shard_map/reduce_scatter | solution.py:31
  508.6 1.2 add_convert_fusion.1
  510.0 1.6 reshape.138
  (96 shorter events, 19.8 us)
Async XLA Ops:
  7.4 16.0 %copy-start.18 = (s32[32]{0:T(128)S(1)}, s32[32]{0:T(128)}, u32[]{:S(2)}) copy-start(s32[32]{0:T(128)} %param.29) | copy-start | bytes 388
  14.3 20.7 %all-to-all-start = ((bf16[32,2,3200]{2,1,0:T(2,128)(2,1)}), bf16[32,2,3200]{2,1,0:T(2,128)(2,1)S(1)}, u32[]{:S(2)}, u32[]{:S(2)}) async-start(bf16[32,2,3200]{2,1,0:T(2,128)(2,1)} %reshape.166), calls=%async_computation | async-start | bytes 819200 | tf_op jit(solution)/shard_map/all_to_all | solution.py:81
  23.3 149.6 %all-gather.6.cloned.1.call-start = ((), (), s32[]{:S(2)}) async-start(), calls=%async_computation.7 | async-start | bytes 3686400 | tf_op jit(solution)/shard_map/all_gather | solution.py:45
  37.1 22.6 %copy-start.9 = (bf16[4,1280]{1,0:T(4,128)(2,1)S(1)}, bf16[4,1280]{1,0:T(4,128)(2,1)}, u32[]{:S(2)}) copy-start(bf16[4,1280]{1,0:T(4,128)(2,1)} %param.21) | copy-start | bytes 30724
  55.4 52.1 %copy-start.8 = (bf16[40,3,128]{2,0,1:T(8,128)(2,1)S(1)}, bf16[40,3,128]{2,0,1:T(8,128)(2,1)}, u32[]{:S(2)}) copy-start(bf16[40,3,128]{2,0,1:T(8,128)(2,1)} %param.19) | copy-start | bytes 92164
  59.7 113.0 %copy-start.10 = (f32[2,128]{1,0:T(2,128)S(1)}, f32[2,128]{1,0:T(2,128)}, u32[]{:S(2)}) copy-start(f32[2,128]{1,0:T(2,128)} %param.20) | copy-start | bytes 3076
  100.3 91.5 %all-to-all-start.3 = ((bf16[128,8,160]{0,2,1:T(8,128)(2,1)}), bf16[128,8,160]{0,2,1:T(8,128)(2,1)S(1)}, u32[]{:S(2)}, u32[]{:S(2)}) async-start(bf16[128,8,160]{0,2,1:T(8,128)(2,1)} %copy.63), calls=%async_computation.3 | async-start | bytes 655360 | tf_op jit(solution)/shard_map/all_to_all | solution.py:139
  172.9 3.9 copy-start.13
  172.9 3.9 copy-start.14
  172.9 2.9 copy-start
  184.4 1.1 copy-start.4
  184.4 1.2 copy-start.5
  186.8 0.7 copy-start.6
  188.6 1.1 copy-start.4
  188.6 1.2 copy-start.5
  191.0 0.7 copy-start.6
  194.4 71.2 %copy-start.2 = (bf16[1280,160]{0,1:T(8,128)(2,1)S(1)}, bf16[1280,160]{0,1:T(8,128)(2,1)}, u32[]{:S(2)}) copy-start(bf16[1280,160]{0,1:T(8,128)(2,1)} %copy.56) | copy-start | bytes 1228804
  194.4 71.2 %copy-start.12 = (f32[160]{0:T(256)S(1)}, f32[160]{0:T(256)}, u32[]{:S(2)}) copy-start(f32[160]{0:T(256)} %param.22) | copy-start | bytes 1924
  194.4 71.2 %all-to-all-start.2 = ((bf16[8,1280,128]{1,2,0:T(8,128)(2,1)}), bf16[8,1280,128]{1,2,0:T(8,128)(2,1)S(1)}, u32[]{:S(2)}, u32[]{:S(2)}) async-start(bf16[8,1280,128]{1,2,0:T(8,128)(2,1)} %broadcast_in_dim.36), calls=%async_computation.2 | async-start | bytes 5242880 | tf_op jit(solution)/shard_map/all_to_all | solution.py:21
  202.7 65.3 %copy-start.7 = (bf16[40,640]{1,0:T(8,128)(2,1)S(1)}, bf16[40,640]{1,0:T(8,128)(2,1)}, u32[]{:S(2)}) copy-start(bf16[40,640]{1,0:T(8,128)(2,1)} %param.25) | copy-start | bytes 153604
  202.7 111.1 %all-gather.10.cloned.1.call-start = ((), (), s32[]{:S(2)}) async-start(), calls=%async_computation.11 | async-start | bytes 2027520 | tf_op jit(solution)/shard_map/all_gather | solution.py:151
  203.3 208.5 %all-gather.8.cloned.1.call-start = ((), (), s32[]{:S(2)}) async-start(), calls=%async_computation.8 | async-start | bytes 3686400 | tf_op jit(solution)/shard_map/all_gather | solution.py:45
  269.4 146.2 %all-to-all-start.4 = ((bf16[32,40,640]{2,1,0:T(8,128)(2,1)}), bf16[32,40,640]{2,1,0:T(8,128)(2,1)}, u32[]{:S(2)}, u32[]{:S(2)}) async-start(bf16[32,40,640]{2,1,0:T(8,128)(2,1)} %broadcast_in_dim.37), calls=%async_computation.4 | async-start | bytes 3276800 | tf_op jit(solution)/shard_map/all_to_all | solution.py:21
  282.0 190.6 %reduce-scatter.3.cloned.1.call-start = ((), (), s32[]{:S(2)}) async-start(), calls=%async_computation.9 | async-start | bytes 4096000 | tf_op jit(solution)/shard_map/reduce_scatter | solution.py:31
  317.9 97.7 %copy-start.15 = (f32[1280]{0:T(1024)S(1)}, f32[1280]{0:T(1024)}, u32[]{:S(2)}) copy-start(f32[1280]{0:T(1024)} %param.24) | copy-start | bytes 15364
  317.9 97.7 %copy-start.16 = (f32[1280]{0:T(1024)S(1)}, f32[1280]{0:T(1024)}, u32[]{:S(2)}) copy-start(f32[1280]{0:T(1024)} %param.23) | copy-start | bytes 15364
  317.9 97.7 %copy-start.17 = (f32[640]{0:T(1024)S(1)}, f32[640]{0:T(1024)}, u32[]{:S(2)}) copy-start(f32[640]{0:T(1024)} %param.26) | copy-start | bytes 7684
  411.8 2.9 copy-start.1
  435.2 73.3 %copy-start.3 = (bf16[1280,160]{0,1:T(8,128)(2,1)S(1)}, bf16[1280,160]{0,1:T(8,128)(2,1)}, u32[]{:S(2)}) copy-start(bf16[1280,160]{0,1:T(8,128)(2,1)} %fusion.46) | copy-start | bytes 1228804
  435.2 73.3 %copy-start.11 = (f32[160]{0:T(256)S(1)}, f32[160]{0:T(256)}, u32[]{:S(2)}) copy-start(f32[160]{0:T(256)} %param.28) | copy-start | bytes 1924
  435.3 73.3 %reduce-scatter.5.cloned.1.call-start = ((), (), s32[]{:S(2)}) async-start(), calls=%async_computation.10 | async-start | bytes 1228800 | tf_op jit(solution)/shard_map/reduce_scatter | solution.py:31
Sparse Core Ops, SparseCore 0:
  59.8 99.7 all-gather.5
  435.4 37.2 reduce-scatter.2
Sparse Core Ops, SparseCore 1:
  205.1 108.7 all-gather.9
  316.3 95.4 all-gather.7
  472.8 35.7 reduce-scatter.4
where the time goes:
time: 528 us; the launch traced here: 519 us
  waiting for transfers between devices  272 us (52%)
  blocking collectives  121 us (23%)
  starting transfers between devices  37.3 us (7%)
  local copies, waits for them, and re-layouts  29.5 us (6%)
  matrix products  24.3 us (5%)
  other arithmetic  19.4 us (4%)
  between operations  15.5 us (3%)
    all_gather x2, waiting for transfers between devices, normalize(): whole_rows = lax.all_gather(residual_in, HEAD, axis=1, tiled=True)  93.8 us
    reduce_scatter x2, waiting for transfers between devices, own_rows(): total = lax.psum_scatter(total, axis, scatter_dimension=0, tiled=True)  73.2 us
    all_gather x1, blocking collectives, on_device(): weight_piece = lax.all_gather(qkv_weight, 'dp', axis=0, tiled=True)  64.6 us
    all_to_all x2, waiting for transfers between devices, sent_to_all(): return lax.all_to_all(copies, axis, split_axis=0, concat_axis=0, tiled=True)  61.5 us
    all_gather x1, blocking collectives, on_device(): output_rows = lax.all_gather(out_weight, 'dp', axis=0, tiled=True)  38.8 us
    all_gather x1, waiting for transfers between devices, on_device(): down_rows = lax.all_gather(fc2_weight, 'dp', axis=0, tiled=True)  31.7 us
    all_to_all x2, starting transfers between devices, sent_to_all(): return lax.all_to_all(copies, axis, split_axis=0, concat_axis=0, tiled=True)  20.9 us
    all_to_all x1, blocking collectives, regroup(): lax.all_to_all(picked, 'dp', split_axis=0, concat_axis=0, tiled=True)  17.8 us
  transfers between devices with their start and end apart: 9, of which 6 were waited for; matrix products, arithmetic and copies ran while one was open for 6% of the time, Pallas kernels for 0%

commit v1 on v0

--- a/solution.py
+++ b/solution.py
@@ -42,7 +42,8 @@
 
 
 def normalize(residual_in, gain_row, shift_row):
-    whole_rows = lax.all_gather(residual_in, HEAD, axis=1, tiled=True)
+    parts = lax.all_gather(residual_in, HEAD, axis=0, tiled=False)
+    whole_rows = jnp.concatenate(parts, axis=1)
     return layer_norm(whole_rows, gain_row, shift_row)
 
 

time: 528 us -> 533 us (level)
  waiting for transfers between devices: 272 us -> 261 us
  local copies, waits for them, and re-layouts: 29.5 us -> 36.6 us
  other arithmetic: 19.4 us -> 25.8 us
    all_to_all x2, waiting for transfers between devices: 61.5 us -> 51.3 us  [sent_to_all(): return lax.all_to_all(copies, axis, split_axis=0, concat_axis=0, tiled=True)]
    convert_element_type x0 -> x4, other arithmetic: none -> 6.49 us  [the longest x1 3.16 us: on_device(): carried = residual_in.astype(jnp.float32) + out_bias]
  transfers between devices with their start and end apart: 9 -> 9, of which waited for: 6 -> 6; matrix products, arithmetic and copies ran while one was open for 6% -> 9% of each run, Pallas kernels for 0% -> 0%
where the time goes in v1:
time: 533 us; the launch traced here: 525 us
  waiting for transfers between devices  261 us (49%)
  blocking collectives  123 us (23%)
  starting transfers between devices  38.8 us (7%)
  local copies, waits for them, and re-layouts  36.6 us (7%)
  other arithmetic  25.8 us (5%)
  matrix products  23.7 us (4%)
  between operations  15.8 us (3%)
    all_gather x2, waiting for transfers between devices, normalize(): parts = lax.all_gather(residual_in, HEAD, axis=0, tiled=False)  94.7 us
    reduce_scatter x2, waiting for transfers between devices, own_rows(): total = lax.psum_scatter(total, axis, scatter_dimension=0, tiled=True)  73.1 us
    all_gather x1, blocking collectives, on_device(): weight_piece = lax.all_gather(qkv_weight, 'dp', axis=0, tiled=True)  66.7 us
    all_to_all x2, waiting for transfers between devices, sent_to_all(): return lax.all_to_all(copies, axis, split_axis=0, concat_axis=0, tiled=True)  51.3 us
    all_gather x1, blocking collectives, on_device(): output_rows = lax.all_gather(out_weight, 'dp', axis=0, tiled=True)  38.8 us
    all_gather x1, waiting for transfers between devices, on_device(): down_rows = lax.all_gather(fc2_weight, 'dp', axis=0, tiled=True)  29.8 us
    all_to_all x2, starting transfers between devices, sent_to_all(): return lax.all_to_all(copies, axis, split_axis=0, concat_axis=0, tiled=True)  22.4 us
    all_to_all x1, blocking collectives, regroup(): lax.all_to_all(picked, 'dp', split_axis=0, concat_axis=0, tiled=True)  17.8 us
  transfers between devices with their start and end apart: 9, of which 6 were waited for; matrix products, arithmetic and copies ran while one was open for 9% of the time, Pallas kernels for 0%

profile of v1, /device:TPU:2, one launch (start us, length us, event | category | flops | bytes accessed | tf_op | source)
XLA Modules:
  0.0 524.7 jit_solution(17536133072313232044)
XLA Ops:
  7.4 2.4 all_to_all.38
  10.4 3.1 reduce.22
  14.3 9.1 %all-to-all-start = ((bf16[32,2,3200]{2,1,0:T(2,128)(2,1)}), bf16[32,2,3200]{2,1,0:T(2,128)(2,1)S(1)}, u32[]{:S(2)}, u32[]{:S(2)}) async-start(bf16[32,2,3200]{2,1,0:T(2,128)(2,1)} %reshape.227), calls=%async_computation | async-start | bytes 819200 | tf_op jit(solution)/shard_map/all_to_all | solution.py:82
  23.8 11.2 %all-to-all-done = bf16[32,2,3200]{2,1,0:T(2,128)(2,1)S(1)} async-done(((bf16[32,2,3200]{2,1,0:T(2,128)(2,1)}), bf16[32,2,3200]{2,1,0:T(2,128)(2,1)S(1)}, u32[]{:S(2)}, u32[]{:S(2)}) %all-to-all-start) | async-done | bytes 409632 | tf_op jit(solution)/shard_map/all_to_all | solution.py:82
  37.4 17.8 %all_to_all.44 = bf16[32,2,3200]{2,1,0:T(2,128)(2,1)S(1)} all-to-all(bf16[32,2,3200]{2,1,0:T(2,128)(2,1)S(1)} %reshape.229), channel_id=1, replica_groups=mesh['dp'=32,'head_0'=4,'head_1'=2] {'dp'}, dimensions={0} | all-to-all | bytes 819200 | tf_op jit(solution)/shard_map/all_to_all | solution.py:84
  55.6 2.4 reduce.11
  59.8 38.8 %all-gather.1 = bf16[32,4,1280]{2,1,0:T(4,128)(2,1)S(1)} all-gather(bf16[1,4,1280]{2,1,0:T(4,128)(2,1)S(1)} %bitcast.113), channel_id=1, replica_groups=mesh['dp'=32,'head_0'=4,'head_1'=2] {'dp'}, dimensions={0}, use_global_device_ids=true | all-gather | bytes 337920 | tf_op jit(solution)/shard_map/all_gather | solution.py:136
  100.4 7.2 %all-to-all-start.3 = ((bf16[128,8,160]{0,2,1:T(8,128)(2,1)}), bf16[128,8,160]{0,2,1:T(8,128)(2,1)}, u32[]{:S(2)}, u32[]{:S(2)}) async-start(bf16[128,8,160]{0,2,1:T(8,128)(2,1)} %copy.68), calls=%async_computation.3 | async-start | bytes 655360 | tf_op jit(solution)/shard_map/all_to_all | solution.py:140
  107.8 66.7 %all_gather.19 = bf16[1280,3,128]{2,0,1:T(8,128)(2,1)S(1)} all-gather(bf16[40,3,128]{2,0,1:T(8,128)(2,1)S(1)} %copy-done.7), channel_id=1, replica_groups=mesh['dp'=32,'head_0'=4,'head_1'=2] {'dp'}, dimensions={0}, use_global_device_ids=true | all-gather | bytes 1013760 | tf_op jit(solution)/shard_map/all_gather | solution.py:123
  175.3 2.6 convert_reduce_fusion
  180.5 1.5 fusion.31
  183.3 1.5 copy.67
  186.0 2.4 fusion.33
  188.4 8.4 %while.10 = (s32[]{:T(128)}, bf16[2,1280,64]{1,2,0:T(8,128)(2,1)}, bf16[2,1280,64]{2,1,0:T(8,128)(2,1)S(1)}, bf16[2,1280,64]{2,1,0:T(8,128)(2,1)S(1)}, bf16[2,1280,64]{2,1,0:T(8,128)(2,1)}, /*index=5*/s32[]{:T(128)}) while((s32[]{:T(128)}, bf16[2,1280,64]{1,2,0:T(8,128)(2,1)}, bf16[2,1280,64]{2,1,0:T(8,128)(2,1)S(1)}, ...), condition=%wide.region_7.8_spmd, body=%wide.region_4.7_spmd.sunk | while | flops 429340160 | bytes 24773784 | solution.py:62
  196.8 2.6 broadcast_in_dim.36
  199.5 7.9 %all-to-all-start.2 = ((bf16[8,1280,128]{1,2,0:T(8,128)(2,1)}), bf16[8,1280,128]{1,2,0:T(8,128)(2,1)S(1)}, u32[]{:S(2)}, u32[]{:S(2)}) async-start(bf16[8,1280,128]{1,2,0:T(8,128)(2,1)} %broadcast_in_dim.36), calls=%async_computation.2 | async-start | bytes 5242880 | tf_op jit(solution)/shard_map/all_to_all | solution.py:21
  208.0 1.8 copy.69
  209.8 3.2 convert_reduce_fusion.2
  213.0 3.0 reshape.195
  216.0 1.7 copy.61
  217.6 51.3 %all-to-all-done.2 = bf16[8,1280,128]{1,2,0:T(8,128)(2,1)S(1)} async-done(((bf16[8,1280,128]{1,2,0:T(8,128)(2,1)}), bf16[8,1280,128]{1,2,0:T(8,128)(2,1)S(1)}, u32[]{:S(2)}, u32[]{:S(2)}) %all-to-all-start.2) | async-done | bytes 2621472 | tf_op jit(solution)/shard_map/all_to_all | solution.py:21
  269.0 2.3 fusion.30
  272.7 14.5 %all-to-all-start.4 = ((bf16[32,40,640]{2,1,0:T(8,128)(2,1)}), bf16[32,40,640]{2,1,0:T(8,128)(2,1)}, u32[]{:S(2)}, u32[]{:S(2)}) async-start(bf16[32,40,640]{2,1,0:T(8,128)(2,1)} %broadcast_in_dim.37), calls=%async_computation.4 | async-start | bytes 3276800 | tf_op jit(solution)/shard_map/all_to_all | solution.py:21
  287.4 29.8 %all-gather.11.cloned.1.call-done = bf16[32,20,1280]{2,1,0:T(8,128)(2,1)} async-done(((bf16[1,20,1280]{2,1,0:T(8,128)(2,1)}), bf16[32,20,1280]{2,1,0:T(8,128)(2,1)}) %all-gather.11.cloned.1.call-update) | async-done | bytes 1638416 | tf_op jit(solution)/shard_map/all_gather | solution.py:152
  317.1 3.6 reshape.210
  320.8 94.7 %all-gather.9.cloned.1.call-done = bf16[10240,160]{0,1:T(8,128)(2,1)} async-done(((bf16[1280,160]{0,1:T(8,128)(2,1)}), bf16[10240,160]{0,1:T(8,128)(2,1)}) %all-gather.9.cloned.1.call-update) | async-done | bytes 3276816 | tf_op jit(solution)/shard_map/all_gather | solution.py:45
  415.5 2.6 convert_reduce_fusion.1
  421.2 15.3 %convolution_convert_fusion = bf16[1280,1280]{0,1:T(8,128)(2,1)} fusion(bf16[640,1280]{1,0:T(8,128)(2,1)} %reshape.210, bf16[1280,1280]{0,1:T(8,128)(2,1)S(1)} %bitcast.104, bf16[1280,640]{1,0:T(8,128)(2,1)} %bitcast.28, f32[640]{0:T(1024)S(1)} %copy-done.16), kind=kOutput, calls=%fused_computation.21 | convolution fusion | flops 4250009600 | bytes 9832960 | tf_op jit(solution)/shard_map/dot_general | solution.py:90
  436.5 4.0 copy.78
  440.6 37.2 %reduce-scatter.3.cloned.1.call-done = bf16[2560,160]{0,1:T(8,128)(2,1)} async-done(((bf16[10240,160]{0,1:T(8,128)(2,1)}), bf16[2560,160]{0,1:T(8,128)(2,1)}) %reduce-scatter.3.cloned.1.call-update) | async-done | bytes 819216 | tf_op jit(solution)/shard_map/reduce_scatter | solution.py:31
  477.8 35.8 %reduce-scatter.5.cloned.1.call-done = bf16[1280,160]{0,1:T(8,128)(2,1)} async-done(((bf16[2560,160]{0,1:T(8,128)(2,1)}), bf16[1280,160]{0,1:T(8,128)(2,1)}) %reduce-scatter.5.cloned.1.call-update) | async-done | bytes 409616 | tf_op jit(solution)/shard_map/reduce_scatter | solution.py:31
  515.1 1.6 reshape.194
  (106 shorter events, 29.1 us)
Async XLA Ops:
  7.4 16.1 %copy-start.17 = (s32[32]{0:T(128)S(1)}, s32[32]{0:T(128)}, u32[]{:S(2)}) copy-start(s32[32]{0:T(128)} %param.29) | copy-start | bytes 388
  14.3 20.7 %all-to-all-start = ((bf16[32,2,3200]{2,1,0:T(2,128)(2,1)}), bf16[32,2,3200]{2,1,0:T(2,128)(2,1)S(1)}, u32[]{:S(2)}, u32[]{:S(2)}) async-start(bf16[32,2,3200]{2,1,0:T(2,128)(2,1)} %reshape.227), calls=%async_computation | async-start | bytes 819200 | tf_op jit(solution)/shard_map/all_to_all | solution.py:82
  23.4 151.9 %all-gather.7.cloned.1.call-start = ((), (), s32[]{:S(2)}) async-start(), calls=%async_computation.7 | async-start | bytes 3686400 | tf_op jit(solution)/shard_map/all_gather | solution.py:45
  37.3 22.6 %copy-start.8 = (bf16[4,1280]{1,0:T(4,128)(2,1)S(1)}, bf16[4,1280]{1,0:T(4,128)(2,1)}, u32[]{:S(2)}) copy-start(bf16[4,1280]{1,0:T(4,128)(2,1)} %param.21) | copy-start | bytes 30724
  55.5 52.1 %copy-start.9 = (f32[1280]{0:T(1024)S(1)}, f32[1280]{0:T(1024)}, u32[]{:S(2)}) copy-start(f32[1280]{0:T(1024)} %param.18) | copy-start | bytes 15364
  55.5 52.2 %copy-start.10 = (f32[1280]{0:T(1024)S(1)}, f32[1280]{0:T(1024)}, u32[]{:S(2)}) copy-start(f32[1280]{0:T(1024)} %param.17) | copy-start | bytes 15364
  55.5 52.3 %copy-start.7 = (bf16[40,3,128]{2,0,1:T(8,128)(2,1)S(1)}, bf16[40,3,128]{2,0,1:T(8,128)(2,1)}, u32[]{:S(2)}) copy-start(bf16[40,3,128]{2,0,1:T(8,128)(2,1)} %param.19) | copy-start | bytes 92164
  59.8 115.3 %copy-start.14 = (f32[2,128]{1,0:T(2,128)S(1)}, f32[2,128]{1,0:T(2,128)}, u32[]{:S(2)}) copy-start(f32[2,128]{1,0:T(2,128)} %param.20) | copy-start | bytes 3076
  100.4 96.4 %all-to-all-start.3 = ((bf16[128,8,160]{0,2,1:T(8,128)(2,1)}), bf16[128,8,160]{0,2,1:T(8,128)(2,1)}, u32[]{:S(2)}, u32[]{:S(2)}) async-start(bf16[128,8,160]{0,2,1:T(8,128)(2,1)} %copy.68), calls=%async_computation.3 | async-start | bytes 655360 | tf_op jit(solution)/shard_map/all_to_all | solution.py:140
  175.3 2.9 copy-start
  189.5 1.1 copy-start.3
  189.5 1.2 copy-start.4
  191.9 0.7 copy-start.5
  193.7 1.1 copy-start.3
  193.7 1.2 copy-start.4
  196.1 0.7 copy-start.5
  199.5 69.5 %all-to-all-start.2 = ((bf16[8,1280,128]{1,2,0:T(8,128)(2,1)}), bf16[8,1280,128]{1,2,0:T(8,128)(2,1)S(1)}, u32[]{:S(2)}, u32[]{:S(2)}) async-start(bf16[8,1280,128]{1,2,0:T(8,128)(2,1)} %broadcast_in_dim.36), calls=%async_computation.2 | async-start | bytes 5242880 | tf_op jit(solution)/shard_map/all_to_all | solution.py:21
  207.4 109.8 %all-gather.11.cloned.1.call-start = ((), (), s32[]{:S(2)}) async-start(), calls=%async_computation.11 | async-start | bytes 2027520 | tf_op jit(solution)/shard_map/all_gather | solution.py:152
  207.9 207.5 %all-gather.9.cloned.1.call-start = ((), (), s32[]{:S(2)}) async-start(), calls=%async_computation.10 | async-start | bytes 3686400 | tf_op jit(solution)/shard_map/all_gather | solution.py:45
  208.0 61.0 %copy-start.13 = (f32[160]{0:T(256)S(1)}, f32[160]{0:T(256)}, u32[]{:S(2)}) copy-start(f32[160]{0:T(256)} %param.22) | copy-start | bytes 1924
  216.0 55.4 %copy-start.6 = (bf16[40,640]{1,0:T(8,128)(2,1)S(1)}, bf16[40,640]{1,0:T(8,128)(2,1)}, u32[]{:S(2)}) copy-start(bf16[40,640]{1,0:T(8,128)(2,1)} %param.25) | copy-start | bytes 153604
  271.3 15.9 %copy-start.11 = (f32[1280]{0:T(1024)S(1)}, f32[1280]{0:T(1024)}, u32[]{:S(2)}) copy-start(f32[1280]{0:T(1024)} %param.24) | copy-start | bytes 15364
  271.3 16.0 %copy-start.12 = (f32[1280]{0:T(1024)S(1)}, f32[1280]{0:T(1024)}, u32[]{:S(2)}) copy-start(f32[1280]{0:T(1024)} %param.23) | copy-start | bytes 15364
  272.7 148.5 %all-to-all-start.4 = ((bf16[32,40,640]{2,1,0:T(8,128)(2,1)}), bf16[32,40,640]{2,1,0:T(8,128)(2,1)}, u32[]{:S(2)}, u32[]{:S(2)}) async-start(bf16[32,40,640]{2,1,0:T(8,128)(2,1)} %broadcast_in_dim.37), calls=%async_computation.4 | async-start | bytes 3276800 | tf_op jit(solution)/shard_map/all_to_all | solution.py:21
  287.2 190.6 %reduce-scatter.3.cloned.1.call-start = ((), (), s32[]{:S(2)}) async-start(), calls=%async_computation.8 | async-start | bytes 4096000 | tf_op jit(solution)/shard_map/reduce_scatter | solution.py:31
  415.5 2.9 copy-start.1
  419.8 1.3 copy-start.16
  440.5 73.2 %copy-start.2 = (bf16[1280,160]{0,1:T(8,128)(2,1)S(1)}, bf16[1280,160]{0,1:T(8,128)(2,1)}, u32[]{:S(2)}) copy-start(bf16[1280,160]{0,1:T(8,128)(2,1)} %fusion.30) | copy-start | bytes 1228804
  440.5 73.2 %copy-start.15 = (f32[160]{0:T(256)S(1)}, f32[160]{0:T(256)}, u32[]{:S(2)}) copy-start(f32[160]{0:T(256)} %param.28) | copy-start | bytes 1924
  440.5 73.1 %reduce-scatter.5.cloned.1.call-start = ((), (), s32[]{:S(2)}) async-start(), calls=%async_computation.9 | async-start | bytes 1228800 | tf_op jit(solution)/shard_map/reduce_scatter | solution.py:31
Sparse Core Ops, SparseCore 0:
  60.0 99.6 all-gather.6
  440.6 37.1 reduce-scatter.2
Sparse Core Ops, SparseCore 1:
  209.7 107.4 all-gather.10
  319.6 95.8 all-gather.8
  477.9 35.7 reduce-scatter.4
